TPU v7x, 32 devices: a whole 2x2x4 slice. The times are simulated.
32 devices in a mesh: gx: 8 (over y, x, core), gy: 4 (over z).
Axes of the slice: x: 2, y: 2, z: 4, core: 2. Of those that a mesh axis runs over, the one named last changes fastest.
Arguments:
- ocean_heat_field: float32 [8, 192, 128, 128], P('gy', 'gx'), may hold values from -6 to 6
- patch_zone: int32 [192], replicated, may hold values from 0 to 31, as said below
- patch_position: int32 [192], replicated, may hold values from 0 to 11, as said below
- quarter_spins: int32 [192], replicated, may hold values from 0 to 3
- zone_patch_tally: int32 [32], P(('gx', 'gy')), may hold values from 0 to 12, as said below
Outputs:
- regional: float32 [8, 32, 12, 128, 128], P(None, ('gx', 'gy'))
Inputs may be any that keep to these rules, and one draw needn't show every extreme that they name: In each aligned group of 24 blocks no more than 6 go to regions of one column patch_zone // 4, and each group has a column with exactly 6. A region receives at most 12 blocks and some region receives exactly 12. `patch_position`: the blocks of one region have distinct slots 0 to zone_patch_tally of that region minus 1, in increasing block order. zone_patch_tally[r] is the number of blocks j with patch_zone[j] = r.
All inputs are finite; a program needn't handle non-finite values.
Results may differ from a plain program's by a relative error of at most 0.00002.
Values sent between devices are 32-bit elements; how exact they have to be, the bound alone decides.
No kernel may reach another device: no remote copies, remote signals or barrier semaphores. Data moves between devices by JAX's collectives and lax.ppermute only.
A program may use at most 128 MiB of HBM per device.

v0:
```python
import jax
import jax.numpy as jnp
from jax import lax
from jax.sharding import PartitionSpec as P


def spin_patches(incoming_patches, turn_codes):
    first_turn = jnp.rot90(incoming_patches, 1, axes=(2, 3))
    half_turn = jnp.rot90(incoming_patches, 2, axes=(2, 3))
    last_turn = jnp.rot90(incoming_patches, 3, axes=(2, 3))
    shaped = turn_codes[None, :, None, None]
    return jnp.where(
        shaped == 0,
        incoming_patches,
        jnp.where(shaped == 1, first_turn, jnp.where(shaped == 2, half_turn, last_turn)),
    )


def rank_within(labels, label_count):
    onehot = (labels[:, None] == jnp.arange(label_count, dtype=jnp.int32)[None, :]).astype(
        jnp.int32
    )
    running = jnp.cumsum(onehot, axis=0) - onehot
    return jnp.sum(running * onehot, axis=1)


def on_device(ocean_heat_field, patch_zone, patch_position, quarter_spins, zone_patch_tally):
    epoch_anomalies = ocean_heat_field.shape[0]
    patch_anomalies = ocean_heat_field.shape[1]
    patch_side_length = ocean_heat_field.shape[2]
    column_count = lax.axis_size("gx")
    row_count = lax.axis_size("gy")
    block_total = patch_zone.shape[0]
    per_peer = 2 * patch_anomalies // column_count
    capacity = 2 * patch_anomalies // row_count
    column = patch_zone // row_count
    block_ids = jnp.arange(block_total, dtype=jnp.int32)
    source_group = block_ids // patch_anomalies
    order_rank = rank_within(source_group * column_count + column, column_count * column_count)
    send_place = column * per_peer + order_rank
    my_column = lax.axis_index("gx")
    first_block = my_column * patch_anomalies
    mine_place = lax.dynamic_slice_in_dim(send_place, first_block, patch_anomalies)
    mine_turns = lax.dynamic_slice_in_dim(quarter_spins, first_block, patch_anomalies)
    incoming_patches = ocean_heat_field
    incoming_patches = spin_patches(incoming_patches, mine_turns)
    outgoing = jnp.zeros(
        (epoch_anomalies, column_count * per_peer, patch_side_length, patch_side_length),
        jnp.float32,
    )
    outgoing = outgoing.at[:, mine_place].set(incoming_patches)
    arrived = lax.all_to_all(outgoing, "gx", split_axis=1, concat_axis=1, tiled=True)
    arrival = source_group * per_peer + order_rank
    row_ids = jnp.arange(row_count, dtype=jnp.int32)[:, None]
    slot_ids = jnp.arange(capacity, dtype=jnp.int32)[None, :]
    targets = ((my_column * row_count + row_ids) * capacity + slot_ids).reshape(-1)
    flat_dest = patch_zone * capacity + patch_position
    matched = flat_dest[None, :] == targets[:, None]
    source = jnp.sum(jnp.where(matched, arrival[None, :] + 1, 0), axis=1) - 1
    present = source >= 0
    picked = jnp.take(arrived, jnp.maximum(source, 0), axis=1)
    picked = jnp.where(present[None, :, None, None], picked, jnp.float32(0.0))
    regional = lax.all_to_all(picked, "gy", split_axis=1, concat_axis=0, tiled=True)
    in_use = jnp.arange(capacity, dtype=jnp.int32) < zone_patch_tally[0]
    regional = jnp.where(in_use[None, :, None, None], regional, jnp.float32(0.0))
    regional = regional - jnp.mean(regional, axis=0, keepdims=True)
    return regional[:, None]


def solution(mesh):
    placed = (P("gy", "gx", None, None), P(), P(), P(), P(("gx", "gy")))
    return jax.shard_map(
        on_device,
        mesh=mesh,
        in_specs=placed,
        out_specs=P(None, ("gx", "gy"), None, None, None),
        check_vma=False,
    )
```

profile of v0, /device:TPU:2, one launch (start us, length us, event | category | flops | bytes accessed | tf_op | source)
XLA Modules:
  0.0 334.6 jit_solution(8710687670302286173)
XLA Ops:
  0.0 2.4 copy.42
  2.4 25.7 %rev.17 = f32[2,24,128,128]{3,2,1,0:T(8,128)} reverse(f32[2,24,128,128]{3,2,1,0:T(8,128)} %param.5), dimensions={2,3} | reverse | bytes 6291456 | tf_op jit(solution)/shard_map/jit(rot90)/jit(_flip)/rev | solution.py:9
  28.1 0.0 copy-start.2
  28.1 15.3 %rev.16 = f32[2,24,128,128]{2,3,1,0:T(8,128)} reverse(f32[2,24,128,128]{2,3,1,0:T(8,128)S(1)} %copy.42), dimensions={3} | reverse | bytes 6291456 | tf_op jit(solution)/shard_map/jit(rot90)/jit(_flip)/rev | solution.py:8
  43.4 17.0 %rev.18 = f32[2,24,128,128]{3,2,1,0:T(8,128)} reverse(f32[2,24,128,128]{3,2,1,0:T(8,128)S(1)} %bitcast.34), dimensions={3} | reverse | bytes 6291456 | tf_op jit(solution)/shard_map/jit(rot90)/jit(_flip)/rev | solution.py:10
  60.4 0.0 copy-done.2
  60.4 0.1 broadcast_compare_fusion.2
  60.5 6.2 %fusion.2 = f32[24,2,128,128]{3,2,0,1:T(8,128)S(1)} fusion(f32[2,24,128,128]{3,2,1,0:T(8,128)} %param.5, f32[2,24,128,128]{2,3,1,0:T(8,128)} %rev.16, f32[2,24,128,128]{3,2,1,0:T(8,128)} %rev.17, f32[2,24,128,128]{3,2,1,0:T(8,128)} %rev.18, pred[24]{0:T(512)(128)(4,1)S(1)} %get-tuple-element.12, pred[24]{0:T(512)(128)(4,1)S(1)} %get-tuple-element.11, ...), kind=kLoop, calls=%fused_computation.8 | loop fusion | flops 2359296 | bytes 15728712 | tf_op jit(solution)/shard_map/jit(_where)/select_n | solution.py:12
  66.7 0.0 copy-start
  66.7 0.0 copy-start.1
  66.7 0.2 copy.44
  66.9 0.4 copy-done
  67.4 0.0 copy-done.1
  67.4 0.6 reduce-window.6
  68.0 0.2 slice_reduce_fusion
  68.3 0.1 bitcast_bitcast_fusion
  68.4 0.1 compare_select_fusion
  68.5 3.5 %broadcast_in_dim.88 = f32[2,48,128,128]{3,2,1,0:T(8,128)} broadcast(f32[]{:T(128)} %constant.72.clone.1), dimensions={} | broadcast | bytes 6291460 | tf_op jit(solution)/shard_map/broadcast_in_dim | solution.py:47
  72.0 6.4 %scatter_fusion = f32[2,48,128,128]{3,2,1,0:T(8,128)} fusion(f32[2,48,128,128]{3,2,1,0:T(8,128)} %broadcast_in_dim.88, s32[24]{0:T(128)S(1)} %compare_select_fusion, f32[24,2,128,128]{3,2,1,0:T(8,128)S(1)} %copy.44), kind=kCustom, calls=%fused_computation.1 | custom fusion | bytes 9437280 | tf_op jit(solution)/shard_map/scatter | solution.py:51
  78.4 6.2 %copy.45 = f32[2,48,128,128]{3,2,0,1:T(8,128)} copy(f32[2,48,128,128]{3,2,1,0:T(8,128)} %scatter_fusion) | data formatting | bytes 12582912 | tf_op jit(solution)/shard_map/scatter | solution.py:51
  84.7 4.7 %all-to-all-start = ((f32[2,48,128,128]{3,2,0,1:T(8,128)}), f32[2,48,128,128]{3,2,0,1:T(8,128)}, u32[]{:S(2)}, u32[]{:S(2)}) async-start(f32[2,48,128,128]{3,2,0,1:T(8,128)} %copy.45), calls=%async_computation | async-start | bytes 12582912 | tf_op jit(solution)/shard_map/all_to_all | solution.py:52
  89.4 0.1 iota_add_fusion
  89.5 0.1 add.94
  89.6 0.2 select_reduce_fusion.1
  89.8 69.4 %all-to-all-done = f32[2,48,128,128]{3,2,0,1:T(8,128)} async-done(((f32[2,48,128,128]{3,2,0,1:T(8,128)}), f32[2,48,128,128]{3,2,0,1:T(8,128)}, u32[]{:S(2)}, u32[]{:S(2)}) %all-to-all-start) | async-done | bytes 6291488 | tf_op jit(solution)/shard_map/all_to_all | solution.py:52
  159.2 6.3 %copy.46 = f32[2,48,128,128]{3,2,1,0:T(8,128)} copy(f32[2,48,128,128]{3,2,0,1:T(8,128)} %all-to-all-done) | data formatting | bytes 12582912 | tf_op jit(solution)/shard_map/all_to_all | solution.py:52
  165.5 6.4 %gather_fusion = f32[48,2,128,128]{3,2,1,0:T(8,128)} fusion(f32[2,48,128,128]{3,2,1,0:T(8,128)} %copy.46, s32[1024]{0:T(1024)S(1)} %pad_clamp_fusion), kind=kCustom, calls=%fused_computation | custom fusion | bytes 12583104 | tf_op jit(solution)/shard_map/jit(_take)/gather | solution.py:61
  171.9 7.0 %select_bitcast_fusion = f32[2,48,128,128]{3,2,0,1:T(8,128)} fusion(f32[48,2,128,128]{3,2,1,0:T(8,128)} %gather_fusion, pred[48]{0:T(512)(128)(4,1)S(1)} %get-tuple-element.14, pred[48]{0:T(512)(128)(4,1)S(1)} %get-tuple-element.13), kind=kLoop, calls=%fused_computation.4 | loop fusion | flops 3145728 | bytes 12583008 | tf_op jit(solution)/shard_map/jit(_where)/select_n | solution.py:62
  178.9 5.7 %all-to-all-start.1 = ((f32[2,48,128,128]{3,2,0,1:T(8,128)}), f32[2,48,128,128]{3,2,0,1:T(8,128)}, u32[]{:S(2)}, u32[]{:S(2)}) async-start(f32[2,48,128,128]{3,2,0,1:T(8,128)} %select_bitcast_fusion), calls=%async_computation.1 | async-start | bytes 12582912 | tf_op jit(solution)/shard_map/all_to_all | solution.py:63
  185.2 138.3 %all-to-all-done.1 = f32[2,48,128,128]{3,2,0,1:T(8,128)} async-done(((f32[2,48,128,128]{3,2,0,1:T(8,128)}), f32[2,48,128,128]{3,2,0,1:T(8,128)}, u32[]{:S(2)}, u32[]{:S(2)}) %all-to-all-start.1) | async-done | bytes 6291488 | tf_op jit(solution)/shard_map/all_to_all | solution.py:63
  323.5 3.2 copy.47
  326.8 0.8 select_reduce_fusion
  327.5 0.1 broadcast_multiply_fusion
  327.6 3.2 copy.48
  330.8 3.7 %fusion = f32[8,1,12,128,128]{4,3,2,0,1:T(8,128)} fusion(f32[4,2,12,128,128]{4,3,2,1,0:T(8,128)S(1)} %copy.48, f32[12,128,128]{2,1,0:T(8,128)S(1)} %broadcast_multiply_fusion, pred[12]{0:T(512)(128)(4,1)S(1)} %iota_compare_fusion.2), kind=kLoop, calls=%fused_computation.3 | loop fusion | flops 3145728 | bytes 13369356 | tf_op jit(solution)/shard_map/sub | solution.py:66
  (12 shorter events, 0.2 us)
Async XLA Ops:
  28.1 32.4 %copy-start.2 = (s32[192]{0:T(256)S(1)}, s32[192]{0:T(256)}, u32[]{:S(2)}) copy-start(s32[192]{0:T(256)} %param.8) | copy-start | bytes 2308
  66.7 0.7 copy-start
  66.7 0.7 copy-start.1
  84.7 74.5 %all-to-all-start = ((f32[2,48,128,128]{3,2,0,1:T(8,128)}), f32[2,48,128,128]{3,2,0,1:T(8,128)}, u32[]{:S(2)}, u32[]{:S(2)}) async-start(f32[2,48,128,128]{3,2,0,1:T(8,128)} %copy.45), calls=%async_computation | async-start | bytes 12582912 | tf_op jit(solution)/shard_map/all_to_all | solution.py:52
  178.9 144.6 %all-to-all-start.1 = ((f32[2,48,128,128]{3,2,0,1:T(8,128)}), f32[2,48,128,128]{3,2,0,1:T(8,128)}, u32[]{:S(2)}, u32[]{:S(2)}) async-start(f32[2,48,128,128]{3,2,0,1:T(8,128)} %select_bitcast_fusion), calls=%async_computation.1 | async-start | bytes 12582912 | tf_op jit(solution)/shard_map/all_to_all | solution.py:63
where the time goes:
time: 337 us; the launch traced here: 335 us
  waiting for transfers between devices  208 us (62%)
  local copies, waits for them, and re-layouts  96.6 us (29%)
  other arithmetic  19 us (6%)
  starting transfers between devices  10.4 us (3%)
    all_to_all x1, waiting for transfers between devices, on_device(): lax.all_to_all(picked, 'gy', split_axis=1, concat_axis=0, tiled=True)  138 us
    all_to_all x1, waiting for transfers between devices, on_device(): lax.all_to_all(outgoing, 'gx', split_axis=1, concat_axis=1, tiled=True)  69.4 us
    rev x1, local copies, waits for them, and re-layouts, spin_patches(): half_turn = jnp.rot90(incoming_patches, 2, axes=(2, 3))  25.7 us
    rev x1, local copies, waits for them, and re-layouts, spin_patches(): last_turn = jnp.rot90(incoming_patches, 3, axes=(2, 3))  17 us
    rev x1, local copies, waits for them, and re-layouts, spin_patches(): first_turn = jnp.rot90(incoming_patches, 1, axes=(2, 3))  15.3 us
    scatter x2, local copies, waits for them, and re-layouts, on_device(): outgoing = outgoing.at[:, mine_place].set(incoming_patches)  12.7 us
    select_n x1, other arithmetic, on_device(): picked = jnp.where(present[None, :, None, None], picked, jnp.float32(0.0))  7.01 us
  transfers between devices with their start and end apart: 2, of which 2 were waited for; matrix products, arithmetic and copies ran while one was open for 0% of the time, Pallas kernels for 0%

commit v1 on v0

v1 whole, which is shorter than its diff:
```python
import functools

import jax
import jax.numpy as jnp
from jax import lax
from jax.experimental import pallas as pl
from jax.experimental.pallas import tpu as pltpu
from jax.sharding import PartitionSpec as P

CHUNKS = 4

SMEM = pl.BlockSpec(memory_space=pltpu.SMEM)
VMEM = pl.BlockSpec(memory_space=pltpu.VMEM)


def select_dot(a, b, contract_b):
    return lax.dot_general(
        a,
        b,
        (((1,), (contract_b,)), ((), ())),
        precision=lax.Precision.HIGHEST,
        preferred_element_type=jnp.float32,
    )


def pack_kernel(first_row, rows, places, turns, x_ref, out_ref):
    steps, blocks, side, _ = x_ref.shape
    row = lax.broadcasted_iota(jnp.int32, (rows, side), 0) + first_row
    lane = lax.broadcasted_iota(jnp.int32, (rows, side), 1)
    keep = (lane == row).astype(jnp.float32)
    flip = (lane == side - 1 - row).astype(jnp.float32)
    whole_row = lax.broadcasted_iota(jnp.int32, (side, side), 0)
    whole_lane = lax.broadcasted_iota(jnp.int32, (side, side), 1)
    mirror = (whole_lane == side - 1 - whole_row).astype(jnp.float32)

    def one(j, carry):
        place = places[j]
        turn = turns[j]

        @pl.when(turn == 0)
        def _():
            for t in range(steps):
                out_ref[place, t] = x_ref[t, j, pl.ds(first_row, rows), :]

        @pl.when(turn == 1)
        def _():
            for t in range(steps):
                out_ref[place, t] = select_dot(flip, x_ref[t, j], 1)

        @pl.when(turn == 2)
        def _():
            for t in range(steps):
                out_ref[place, t] = select_dot(select_dot(flip, x_ref[t, j], 0), mirror, 0)

        @pl.when(turn == 3)
        def _():
            for t in range(steps):
                out_ref[place, t] = select_dot(select_dot(keep, x_ref[t, j], 1), mirror, 0)

        return carry

    lax.fori_loop(0, blocks, one, 0)


def pick_kernel(source, arrived_ref, out_ref):
    def one(s, carry):
        at = source[s]

        @pl.when(at >= 0)
        def _():
            out_ref[s] = arrived_ref[at]

        return carry

    lax.fori_loop(0, out_ref.shape[0], one, 0)


def center_kernel(tally, *refs):
    z_ref, out_ref = refs[0], refs[-1]
    groups, slots, steps, rows, side = z_ref.shape
    first_slot = pl.program_id(0) * slots
    for s in range(slots):
        used = first_slot + s < tally[0]

        @pl.when(used)
        def _():
            values = z_ref[:, s].reshape(groups * steps, rows, side)
            mean = jnp.sum(values, axis=0, keepdims=True) * (1.0 / (groups * steps))
            out_ref[:, 0, s] = values - mean

        @pl.when(jnp.logical_not(used))
        def _():
            out_ref[:, 0, s] = jnp.zeros((groups * steps, rows, side), jnp.float32)


def on_device(ocean_heat_field, patch_zone, patch_position, quarter_spins, zone_patch_tally):
    steps, patches, side, _ = ocean_heat_field.shape
    columns = lax.axis_size("gx")
    row_count = lax.axis_size("gy")
    per_peer = 2 * patches // columns
    capacity = 2 * patches // row_count
    rows = side // CHUNKS
    me = lax.axis_index("gx")

    column = (patch_zone // row_count).reshape(columns, patches)
    same = column[:, :, None] == column[:, None, :]
    earlier = jnp.arange(patches)[None, None, :] < jnp.arange(patches)[None, :, None]
    rank = jnp.sum((same & earlier).astype(jnp.int32), axis=2)
    my_column = lax.dynamic_index_in_dim(column, me, 0, keepdims=False)
    my_rank = lax.dynamic_index_in_dim(rank, me, 0, keepdims=False)
    places = my_column * per_peer + my_rank
    turns = lax.dynamic_slice_in_dim(quarter_spins, me * patches, patches)
    arrival = (jnp.arange(columns, dtype=jnp.int32)[:, None] * per_peer + rank).reshape(-1)
    first_target = me * row_count * capacity
    targets = first_target + jnp.arange(row_count * capacity, dtype=jnp.int32)
    flat_dest = patch_zone * capacity + patch_position
    matched = flat_dest[None, :] == targets[:, None]
    source = jnp.sum(jnp.where(matched, arrival[None, :] + 1, 0), axis=1) - 1

    per_step = capacity // 3
    out_shape = jax.ShapeDtypeStruct(
        (steps * row_count, 1, capacity, side, side), jnp.float32
    )
    regional = None
    for k in range(CHUNKS):
        packed = pl.pallas_call(
            functools.partial(pack_kernel, k * rows, rows),
            out_shape=jax.ShapeDtypeStruct(
                (columns * per_peer, steps, rows, side), jnp.float32
            ),
            in_specs=[SMEM, SMEM, VMEM],
            out_specs=VMEM,
            name=f"pack{k}",
        )(places, turns, ocean_heat_field)
        arrived = lax.all_to_all(packed, "gx", split_axis=0, concat_axis=0, tiled=True)
        picked = pl.pallas_call(
            pick_kernel,
            out_shape=jax.ShapeDtypeStruct(
                (row_count * capacity, steps, rows, side), jnp.float32
            ),
            in_specs=[SMEM, VMEM],
            out_specs=VMEM,
            name="pick",
        )(source, arrived)
        timed = lax.all_to_all(picked, "gy", split_axis=0, concat_axis=0, tiled=True)
        timed = timed.reshape(row_count, capacity, steps, rows, side)
        operands = (zone_patch_tally, timed) + (() if k == 0 else (regional,))
        regional = pl.pallas_call(
            center_kernel,
            grid=(capacity // per_step,),
            out_shape=out_shape,
            in_specs=[
                SMEM,
                pl.BlockSpec((row_count, per_step, steps, rows, side), lambda i: (0, i, 0, 0, 0)),
            ]
            + ([] if k == 0 else [pl.BlockSpec(memory_space=pl.ANY)]),
            out_specs=pl.BlockSpec(
                (steps * row_count, 1, per_step, rows, side),
                functools.partial(lambda k, i: (0, 0, i, k, 0), k),
            ),
            input_output_aliases={} if k == 0 else {2: 0},
            name=f"center{k}",
        )(*operands)
    return regional


def solution(mesh):
    placed = (P("gy", "gx", None, None), P(), P(), P(), P(("gx", "gy")))
    return jax.shard_map(
        on_device,
        mesh=mesh,
        in_specs=placed,
        out_specs=P(None, ("gx", "gy"), None, None, None),
        check_vma=False,
    )
```

time: 337 us -> 291 us (0.86)
  local copies, waits for them, and re-layouts: 96.6 us -> 9.52 us
  Pallas kernels: 0 us -> 83.7 us
  waiting for transfers between devices: 208 us -> 157 us
  starting transfers between devices: 10.4 us -> 36.7 us
  other arithmetic: 19 us -> 2.4 us
    pallas_call x0 -> x12, Pallas kernels: none -> 83.7 us  [the longest x4 56.9 us: on_device(): pl.pallas_call(functools.partial(pack_kernel, k * rows, rows), out_shape=...]
    rev x3 -> x0, local copies, waits for them, and re-layouts: 58.1 us -> none  [the longest x1 25.7 us: spin_patches(): half_turn = jnp.rot90(incoming_patches, 2, axes=(2, 3))]
    all_to_all x2 -> x8, waiting for transfers between devices: 208 us -> 157 us  [the longest x4 126 us: on_device(): lax.all_to_all(picked, 'gy', split_axis=0, concat_axis=0, tiled=True)]
    all_to_all x2 -> x8, starting transfers between devices: 10.4 us -> 36.7 us  [the longest x4 19.7 us: on_device(): lax.all_to_all(packed, 'gx', split_axis=0, concat_axis=0, tiled=True)]
    select_n x3 -> x0, other arithmetic: 13.3 us -> none  [the longest x1 7.01 us: on_device(): picked = jnp.where(present[None, :, None, None], picked, jnp.float32(0.0))]
    all_to_all x3 -> x0, local copies, waits for them, and re-layouts: 12.7 us -> none  [the longest x2 6.41 us: on_device(): lax.all_to_all(picked, 'gy', split_axis=1, concat_axis=0, tiled=True)]
    scatter x2 -> x0, local copies, waits for them, and re-layouts: 12.7 us -> none  [on_device(): outgoing = outgoing.at[:, mine_place].set(incoming_patches)]
    gather x1 -> x0, local copies, waits for them, and re-layouts: 6.39 us -> none  [on_device(): picked = jnp.take(arrived, jnp.maximum(source, 0), axis=1)]
  transfers between devices with their start and end apart: 2 -> 8, of which waited for: 2 -> 8; matrix products, arithmetic and copies ran while one was open for 0% -> 0% of each run, Pallas kernels for 0% -> 23%
where the time goes in v1:
time: 291 us; the launch traced here: 290 us
  waiting for transfers between devices  157 us (54%)
  Pallas kernels  83.7 us (29%)
  starting transfers between devices  36.7 us (13%)
  local copies, waits for them, and re-layouts  9.52 us (3%)
    all_to_all x4, waiting for transfers between devices, on_device(): lax.all_to_all(picked, 'gy', split_axis=0, concat_axis=0, tiled=True)  126 us
    pallas_call x4, Pallas kernels, on_device(): pl.pallas_call(functools.partial(pack_kernel, k * rows, rows), out_shape=...  56.9 us
    all_to_all x4, waiting for transfers between devices, on_device(): lax.all_to_all(packed, 'gx', split_axis=0, concat_axis=0, tiled=True)  31.2 us
    all_to_all x4, starting transfers between devices, on_device(): lax.all_to_all(packed, 'gx', split_axis=0, concat_axis=0, tiled=True)  19.7 us
    all_to_all x4, starting transfers between devices, on_device(): lax.all_to_all(picked, 'gy', split_axis=0, concat_axis=0, tiled=True)  17 us
    pallas_call x4, Pallas kernels, on_device(): pl.pallas_call(center_kernel, grid=(capacity // per_step,), out_shape=out...  13.8 us
    pallas_call x4, Pallas kernels, on_device(): pl.pallas_call(pick_kernel, out_shape=jax.ShapeDtypeStruct((row_count * c...  13.1 us
    unnamed x16, local copies, waits for them, and re-layouts  8.12 us
  transfers between devices with their start and end apart: 8, of which 8 were waited for; matrix products, arithmetic and copies ran while one was open for 0% of the time, Pallas kernels for 23%

profile of v1, /device:TPU:2, one launch (start us, length us, event | category | flops | bytes accessed | tf_op | source)
XLA Modules:
  0.0 290.1 jit_solution(8655580384670852309)
XLA Ops:
  0.0 0.7 multiply_add_fusion
  0.7 0.1 eq.31
  0.8 1.2 dynamic_slice.12.turns
  2.0 0.3 convert_reduce_fusion
  2.3 0.6 add_bitcast_fusion.places
  2.9 14.2 %pack0.1 = f32[48,2,32,128]{3,2,1,0:T(8,128)} custom-call(s32[24]{0:T(128)} %add_bitcast_fusion.places, s32[24]{0:T(128)} %dynamic_slice.12.turns, f32[2,24,128,128]{3,2,1,0:T(8,128)} %x_ref.7), custom_call_target="tpu_custom_call" | custom-call | tf_op jit(solution)/shard_map/pack0/pallas_call | solution.py:126
  17.2 4.6 %all-to-all-start.6 = ((f32[48,2,32,128]{3,2,1,0:T(8,128)}), f32[48,2,32,128]{3,2,1,0:T(8,128)S(1)}, u32[]{:S(2)}, u32[]{:S(2)}) async-start(f32[48,2,32,128]{3,2,1,0:T(8,128)} %pack0.1), calls=%async_computation.6 | async-start | bytes 3145728 | tf_op jit(solution)/shard_map/all_to_all | solution.py:135
  21.8 14.2 %pack1.1 = f32[48,2,32,128]{3,2,1,0:T(8,128)} custom-call(s32[24]{0:T(128)} %add_bitcast_fusion.places, s32[24]{0:T(128)} %dynamic_slice.12.turns, f32[2,24,128,128]{3,2,1,0:T(8,128)} %x_ref.7), custom_call_target="tpu_custom_call" | custom-call | tf_op jit(solution)/shard_map/pack1/pallas_call | solution.py:126
  36.0 5.3 %all-to-all-done.6.arrived_ref = f32[48,2,32,128]{3,2,1,0:T(8,128)S(1)} async-done(((f32[48,2,32,128]{3,2,1,0:T(8,128)}), f32[48,2,32,128]{3,2,1,0:T(8,128)S(1)}, u32[]{:S(2)}, u32[]{:S(2)}) %all-to-all-start.6) | async-done | bytes 1572896 | tf_op jit(solution)/shard_map/all_to_all | solution.py:135
  41.3 0.0 copy-start.3
  41.3 5.0 %all-to-all-start.4 = ((f32[48,2,32,128]{3,2,1,0:T(8,128)}), f32[48,2,32,128]{3,2,1,0:T(8,128)S(1)}, u32[]{:S(2)}, u32[]{:S(2)}) async-start(f32[48,2,32,128]{3,2,1,0:T(8,128)} %pack1.1), calls=%async_computation.4 | async-start | bytes 3145728 | tf_op jit(solution)/shard_map/all_to_all | solution.py:135
  46.3 14.2 %pack2.1 = f32[48,2,32,128]{3,2,1,0:T(8,128)} custom-call(s32[24]{0:T(128)} %add_bitcast_fusion.places, s32[24]{0:T(128)} %dynamic_slice.12.turns, f32[2,24,128,128]{3,2,1,0:T(8,128)} %x_ref.7), custom_call_target="tpu_custom_call" | custom-call | tf_op jit(solution)/shard_map/pack2/pallas_call | solution.py:126
  60.6 0.0 copy-done.3
  60.6 5.3 %all-to-all-done.4.arrived_ref = f32[48,2,32,128]{3,2,1,0:T(8,128)S(1)} async-done(((f32[48,2,32,128]{3,2,1,0:T(8,128)}), f32[48,2,32,128]{3,2,1,0:T(8,128)S(1)}, u32[]{:S(2)}, u32[]{:S(2)}) %all-to-all-start.4) | async-done | bytes 1572896 | tf_op jit(solution)/shard_map/all_to_all | solution.py:135
  65.8 0.0 copy-start.1
  65.8 1.1 copy-done.1
  67.0 5.0 %all-to-all-start.2 = ((f32[48,2,32,128]{3,2,1,0:T(8,128)}), f32[48,2,32,128]{3,2,1,0:T(8,128)S(1)}, u32[]{:S(2)}, u32[]{:S(2)}) async-start(f32[48,2,32,128]{3,2,1,0:T(8,128)} %pack2.1), calls=%async_computation.2 | async-start | bytes 3145728 | tf_op jit(solution)/shard_map/all_to_all | solution.py:135
  72.0 14.2 %pack3.1 = f32[48,2,32,128]{3,2,1,0:T(8,128)} custom-call(s32[24]{0:T(128)} %add_bitcast_fusion.places, s32[24]{0:T(128)} %dynamic_slice.12.turns, f32[2,24,128,128]{3,2,1,0:T(8,128)} %x_ref.7), custom_call_target="tpu_custom_call" | custom-call | tf_op jit(solution)/shard_map/pack3/pallas_call | solution.py:126
  86.2 5.3 %all-to-all-done.2.arrived_ref = f32[48,2,32,128]{3,2,1,0:T(8,128)S(1)} async-done(((f32[48,2,32,128]{3,2,1,0:T(8,128)}), f32[48,2,32,128]{3,2,1,0:T(8,128)S(1)}, u32[]{:S(2)}, u32[]{:S(2)}) %all-to-all-start.2) | async-done | bytes 1572896 | tf_op jit(solution)/shard_map/all_to_all | solution.py:135
  91.5 0.0 copy-start
  91.5 1.2 copy-done
  92.7 5.0 %all-to-all-start = ((f32[48,2,32,128]{3,2,1,0:T(8,128)}), f32[48,2,32,128]{3,2,1,0:T(8,128)S(1)}, u32[]{:S(2)}, u32[]{:S(2)}) async-start(f32[48,2,32,128]{3,2,1,0:T(8,128)} %pack3.1), calls=%async_computation | async-start | bytes 3145728 | tf_op jit(solution)/shard_map/all_to_all | solution.py:135
  97.7 0.1 add_add_fusion
  97.8 0.1 add.60
  97.8 0.2 select_reduce_fusion
  98.0 0.5 broadcast_add_fusion.source
  98.6 3.2 %pick.7 = f32[48,2,32,128]{3,2,1,0:T(8,128)} custom-call(s32[48]{0:T(128)} %broadcast_add_fusion.source, f32[48,2,32,128]{3,2,1,0:T(8,128)} %copy-done.3), custom_call_target="tpu_custom_call" | custom-call | tf_op jit(solution)/shard_map/pick/pallas_call | solution.py:136
  101.8 15.4 %all-to-all-done.arrived_ref = f32[48,2,32,128]{3,2,1,0:T(8,128)S(1)} async-done(((f32[48,2,32,128]{3,2,1,0:T(8,128)}), f32[48,2,32,128]{3,2,1,0:T(8,128)S(1)}, u32[]{:S(2)}, u32[]{:S(2)}) %all-to-all-start) | async-done | bytes 1572896 | tf_op jit(solution)/shard_map/all_to_all | solution.py:135
  117.2 0.0 copy-start.2
  117.2 1.1 copy-done.2
  118.3 6.4 %all-to-all-start.7 = ((f32[48,2,32,128]{3,2,1,0:T(8,128)}), f32[48,2,32,128]{3,2,1,0:T(8,128)S(1)}, u32[]{:S(2)}, u32[]{:S(2)}) async-start(f32[48,2,32,128]{3,2,1,0:T(8,128)} %pick.7), calls=%async_computation.7 | async-start | bytes 3145728 | tf_op jit(solution)/shard_map/all_to_all | solution.py:145
  124.7 3.3 %pick.6 = f32[48,2,32,128]{3,2,1,0:T(8,128)} custom-call(s32[48]{0:T(128)} %broadcast_add_fusion.source, f32[48,2,32,128]{3,2,1,0:T(8,128)} %copy-done.1), custom_call_target="tpu_custom_call" | custom-call | tf_op jit(solution)/shard_map/pick/pallas_call | solution.py:136
  128.0 33.9 %all-to-all-done.7 = f32[48,2,32,128]{3,2,1,0:T(8,128)S(1)} async-done(((f32[48,2,32,128]{3,2,1,0:T(8,128)}), f32[48,2,32,128]{3,2,1,0:T(8,128)S(1)}, u32[]{:S(2)}, u32[]{:S(2)}) %all-to-all-start.7) | async-done | bytes 1572896 | tf_op jit(solution)/shard_map/all_to_all | solution.py:145
  161.9 0.0 copy-start.4
  161.9 1.1 copy-done.4
  163.0 3.6 %all-to-all-start.5 = ((f32[48,2,32,128]{3,2,1,0:T(8,128)}), f32[48,2,32,128]{3,2,1,0:T(8,128)S(1)}, u32[]{:S(2)}, u32[]{:S(2)}) async-start(f32[48,2,32,128]{3,2,1,0:T(8,128)} %pick.6), calls=%async_computation.5 | async-start | bytes 3145728 | tf_op jit(solution)/shard_map/all_to_all | solution.py:145
  166.6 3.3 %pick.5 = f32[48,2,32,128]{3,2,1,0:T(8,128)} custom-call(s32[48]{0:T(128)} %broadcast_add_fusion.source, f32[48,2,32,128]{3,2,1,0:T(8,128)} %copy-done), custom_call_target="tpu_custom_call" | custom-call | tf_op jit(solution)/shard_map/pick/pallas_call | solution.py:136
  169.8 33.2 %all-to-all-done.5 = f32[48,2,32,128]{3,2,1,0:T(8,128)S(1)} async-done(((f32[48,2,32,128]{3,2,1,0:T(8,128)}), f32[48,2,32,128]{3,2,1,0:T(8,128)S(1)}, u32[]{:S(2)}, u32[]{:S(2)}) %all-to-all-start.5) | async-done | bytes 1572896 | tf_op jit(solution)/shard_map/all_to_all | solution.py:145
  203.1 0.0 copy-start.5
  203.1 1.2 copy-done.5
  204.3 3.6 %all-to-all-start.3 = ((f32[48,2,32,128]{3,2,1,0:T(8,128)}), f32[48,2,32,128]{3,2,1,0:T(8,128)S(1)}, u32[]{:S(2)}, u32[]{:S(2)}) async-start(f32[48,2,32,128]{3,2,1,0:T(8,128)} %pick.5), calls=%async_computation.3 | async-start | bytes 3145728 | tf_op jit(solution)/shard_map/all_to_all | solution.py:145
  207.8 3.3 %pick.4 = f32[48,2,32,128]{3,2,1,0:T(8,128)} custom-call(s32[48]{0:T(128)} %broadcast_add_fusion.source, f32[48,2,32,128]{3,2,1,0:T(8,128)} %copy-done.2), custom_call_target="tpu_custom_call" | custom-call | tf_op jit(solution)/shard_map/pick/pallas_call | solution.py:136
  211.1 33.2 %all-to-all-done.3 = f32[48,2,32,128]{3,2,1,0:T(8,128)S(1)} async-done(((f32[48,2,32,128]{3,2,1,0:T(8,128)}), f32[48,2,32,128]{3,2,1,0:T(8,128)S(1)}, u32[]{:S(2)}, u32[]{:S(2)}) %all-to-all-start.3) | async-done | bytes 1572896 | tf_op jit(solution)/shard_map/all_to_all | solution.py:145
  244.3 0.0 copy-start.6
  244.3 1.2 copy-done.6
  245.5 3.6 %all-to-all-start.1 = ((f32[48,2,32,128]{3,2,1,0:T(8,128)}), f32[48,2,32,128]{3,2,1,0:T(8,128)S(1)}, u32[]{:S(2)}, u32[]{:S(2)}) async-start(f32[48,2,32,128]{3,2,1,0:T(8,128)} %pick.4), calls=%async_computation.1 | async-start | bytes 3145728 | tf_op jit(solution)/shard_map/all_to_all | solution.py:145
  249.7 3.5 %center0.1.refs_1_ = f32[8,1,12,128,128]{4,3,2,1,0:T(8,128)} custom-call(s32[1]{0:T(128)S(6)} %copy.12.tally, f32[4,12,2,32,128]{4,3,2,1,0:T(8,128)} %bitcast.6), custom_call_target="tpu_custom_call" | custom-call | tf_op jit(solution)/shard_map/center0/pallas_call | solution.py:148
  253.1 3.4 %center1.1.refs_1_ = f32[8,1,12,128,128]{4,3,2,1,0:T(8,128)} custom-call(s32[1]{0:T(128)S(6)} %copy.12.tally, f32[4,12,2,32,128]{4,3,2,1,0:T(8,128)} %bitcast.7, f32[8,1,12,128,128]{4,3,2,1,0:T(8,128)} %center0.1.refs_1_), custom_call_target="tpu_custom_call", output_to_operand_aliasing={{}: (2, {})} | custom-call | tf_op jit(solution)/shard_map/center1/pallas_call | solution.py:148
  256.6 3.4 %center2.1.refs_1_ = f32[8,1,12,128,128]{4,3,2,1,0:T(8,128)} custom-call(s32[1]{0:T(128)S(6)} %copy.12.tally, f32[4,12,2,32,128]{4,3,2,1,0:T(8,128)} %bitcast.8, f32[8,1,12,128,128]{4,3,2,1,0:T(8,128)} %center1.1.refs_1_), custom_call_target="tpu_custom_call", output_to_operand_aliasing={{}: (2, {})} | custom-call | tf_op jit(solution)/shard_map/center2/pallas_call | solution.py:148
  260.0 25.5 %all-to-all-done.1 = f32[48,2,32,128]{3,2,1,0:T(8,128)S(1)} async-done(((f32[48,2,32,128]{3,2,1,0:T(8,128)}), f32[48,2,32,128]{3,2,1,0:T(8,128)S(1)}, u32[]{:S(2)}, u32[]{:S(2)}) %all-to-all-start.1) | async-done | bytes 1572896 | tf_op jit(solution)/shard_map/all_to_all | solution.py:145
  285.5 0.0 copy-start.7
  285.5 1.2 copy-done.7
  286.7 3.4 %center3.1 = f32[8,1,12,128,128]{4,3,2,1,0:T(8,128)} custom-call(s32[1]{0:T(128)S(6)} %copy.12.tally, f32[4,12,2,32,128]{4,3,2,1,0:T(8,128)} %bitcast.9, f32[8,1,12,128,128]{4,3,2,1,0:T(8,128)} %center2.1.refs_1_), custom_call_target="tpu_custom_call", output_to_operand_aliasing={{}: (2, {})} | custom-call | tf_op jit(solution)/shard_map/center3/pallas_call | solution.py:148
  (3 shorter events, 0.0 us)
Async XLA Ops:
  17.2 24.1 %all-to-all-start.6 = ((f32[48,2,32,128]{3,2,1,0:T(8,128)}), f32[48,2,32,128]{3,2,1,0:T(8,128)S(1)}, u32[]{:S(2)}, u32[]{:S(2)}) async-start(f32[48,2,32,128]{3,2,1,0:T(8,128)} %pack0.1), calls=%async_computation.6 | async-start | bytes 3145728 | tf_op jit(solution)/shard_map/all_to_all | solution.py:135
  41.3 19.3 %copy-start.3 = (f32[48,2,32,128]{3,2,1,0:T(8,128)}, f32[48,2,32,128]{3,2,1,0:T(8,128)S(1)}, u32[]{:S(2)}) copy-start(f32[48,2,32,128]{3,2,1,0:T(8,128)S(1)} %all-to-all-done.6.arrived_ref) | copy-start | bytes 4718596
  41.3 24.5 %all-to-all-start.4 = ((f32[48,2,32,128]{3,2,1,0:T(8,128)}), f32[48,2,32,128]{3,2,1,0:T(8,128)S(1)}, u32[]{:S(2)}, u32[]{:S(2)}) async-start(f32[48,2,32,128]{3,2,1,0:T(8,128)} %pack1.1), calls=%async_computation.4 | async-start | bytes 3145728 | tf_op jit(solution)/shard_map/all_to_all | solution.py:135
  65.8 1.1 copy-start.1
  67.0 24.5 %all-to-all-start.2 = ((f32[48,2,32,128]{3,2,1,0:T(8,128)}), f32[48,2,32,128]{3,2,1,0:T(8,128)S(1)}, u32[]{:S(2)}, u32[]{:S(2)}) async-start(f32[48,2,32,128]{3,2,1,0:T(8,128)} %pack2.1), calls=%async_computation.2 | async-start | bytes 3145728 | tf_op jit(solution)/shard_map/all_to_all | solution.py:135
  91.5 1.2 copy-start
  92.7 24.5 %all-to-all-start = ((f32[48,2,32,128]{3,2,1,0:T(8,128)}), f32[48,2,32,128]{3,2,1,0:T(8,128)S(1)}, u32[]{:S(2)}, u32[]{:S(2)}) async-start(f32[48,2,32,128]{3,2,1,0:T(8,128)} %pack3.1), calls=%async_computation | async-start | bytes 3145728 | tf_op jit(solution)/shard_map/all_to_all | solution.py:135
  117.2 1.1 copy-start.2
  118.3 43.5 %all-to-all-start.7 = ((f32[48,2,32,128]{3,2,1,0:T(8,128)}), f32[48,2,32,128]{3,2,1,0:T(8,128)S(1)}, u32[]{:S(2)}, u32[]{:S(2)}) async-start(f32[48,2,32,128]{3,2,1,0:T(8,128)} %pick.7), calls=%async_computation.7 | async-start | bytes 3145728 | tf_op jit(solution)/shard_map/all_to_all | solution.py:145
  161.9 1.1 copy-start.4
  163.0 40.1 %all-to-all-start.5 = ((f32[48,2,32,128]{3,2,1,0:T(8,128)}), f32[48,2,32,128]{3,2,1,0:T(8,128)S(1)}, u32[]{:S(2)}, u32[]{:S(2)}) async-start(f32[48,2,32,128]{3,2,1,0:T(8,128)} %pick.6), calls=%async_computation.5 | async-start | bytes 3145728 | tf_op jit(solution)/shard_map/all_to_all | solution.py:145
  203.1 1.2 copy-start.5
  204.3 40.1 %all-to-all-start.3 = ((f32[48,2,32,128]{3,2,1,0:T(8,128)}), f32[48,2,32,128]{3,2,1,0:T(8,128)S(1)}, u32[]{:S(2)}, u32[]{:S(2)}) async-start(f32[48,2,32,128]{3,2,1,0:T(8,128)} %pick.5), calls=%async_computation.3 | async-start | bytes 3145728 | tf_op jit(solution)/shard_map/all_to_all | solution.py:145
  244.3 1.2 copy-start.6
  245.5 40.1 %all-to-all-start.1 = ((f32[48,2,32,128]{3,2,1,0:T(8,128)}), f32[48,2,32,128]{3,2,1,0:T(8,128)S(1)}, u32[]{:S(2)}, u32[]{:S(2)}) async-start(f32[48,2,32,128]{3,2,1,0:T(8,128)} %pick.4), calls=%async_computation.1 | async-start | bytes 3145728 | tf_op jit(solution)/shard_map/all_to_all | solution.py:145
  285.5 1.2 copy-start.7
